TPU v7x, 8 devices: a whole 2x2x1 slice. The times are simulated.
8 devices in a mesh: dp: 2 (over y, z), tp: 4 (over x, core).
Axes of the slice: x: 2, y: 2, z: 1, core: 2. Of those that a mesh axis runs over, the one named last changes fastest.
Arguments:
- x: bfloat16 [2048, 4096], P(('dp', 'tp')), parts along dimension 0
- w_gate: bfloat16 [4096, 12800], P(None, 'tp')
- w_up: bfloat16 [4096, 12800], P(None, 'tp')
- w_down: bfloat16 [12800, 4096], P('tp')
Outputs:
- output: bfloat16 [2048, 4096], P(('dp', 'tp')), parts along dimension 0
There are 2 independent parts. A program takes and returns all parts, laid end to end along the dimension named above; an argument that names none is the same for every part.
All inputs are finite; a program needn't handle non-finite values.
Results may differ from a plain program's by a relative error of at most 0.016.
Values are sent between devices in bfloat16 or wider.
A program may use at most 2 GiB of HBM per device.

v0:
```python
import jax
import jax.numpy as jnp
from jax import lax
from jax.sharding import PartitionSpec as P


def solution(mesh):
    def step(x, w_gate, w_up, w_down):
        rows = lax.all_gather(x, "tp", axis=0, tiled=True)
        gate = jnp.dot(rows, w_gate, preferred_element_type=jnp.float32)
        up = jnp.dot(rows, w_up, preferred_element_type=jnp.float32)
        hidden = (jax.nn.silu(gate) * up).astype(jnp.bfloat16)
        term = jnp.dot(hidden, w_down, preferred_element_type=jnp.float32).astype(jnp.bfloat16)
        return lax.psum_scatter(term, "tp", scatter_dimension=0, tiled=True)

    return jax.shard_map(
        step,
        mesh=mesh,
        in_specs=(P(("dp", "tp"), None), P(None, "tp"), P(None, "tp"), P("tp", None)),
        out_specs=P(("dp", "tp"), None),
        check_vma=False,
    )
```

profile of v0, /device:TPU:0, one launch (start us, length us, event | category | flops | bytes accessed | tf_op | source)
XLA Modules:
  0.0 241.7 jit_solution(755029980743479292)
XLA Ops:
  6.5 0.0 all-gather.2.cloned.1.call-start
  6.5 0.7 all-gather.2.cloned.1.call-update
  7.3 0.0 reduce-scatter.2.cloned.1.call-start
  7.3 60.1 %all-gather.2.cloned.1.call-done = bf16[1024,4096]{1,0:T(8,128)(2,1)} async-done(((bf16[256,4096]{1,0:T(8,128)(2,1)}), bf16[1024,4096]{1,0:T(8,128)(2,1)}) %all-gather.2.cloned.1.call-update) | async-done | bytes 8388624 | tf_op jit(solution)/shard_map/all_gather | solution.py:9
  67.4 0.0 copy-start
  67.4 33.1 %fusion.4 = f32[1024,3200]{1,0:T(8,128)S(1)} fusion(bf16[1024,4096]{1,0:T(8,128)(2,1)} %all-gather.2.cloned.1.call-done, bf16[4096,3200]{1,0:T(8,128)(2,1)} %param.5), kind=kOutput, calls=%fused_computation.5 | convolution fusion | flops 26843545600 | bytes 47710208 | tf_op jit(solution)/shard_map/dot_general | solution.py:10
  100.5 0.0 copy-done
  100.5 35.6 %multiply_convert_fusion.clone.6 = bf16[1024,3200]{1,0:T(8,128)(2,1)S(1)} fusion(f32[1024,3200]{1,0:T(8,128)S(1)} %fusion.4, bf16[1024,4096]{1,0:T(8,128)(2,1)S(1)} %copy-done, bf16[4096,3200]{1,0:T(8,128)(2,1)} %param.6), kind=kOutput, calls=%fused_computation.clone.clone.clone.clone.clone.1 | convolution fusion | flops 26863206400 | bytes 54263808 | tf_op jit(solution)/shard_map/dot_general | solution.py:11
  136.1 33.5 %fusion.1 = bf16[1024,4096]{1,0:T(8,128)(2,1)} fusion(bf16[3200,4096]{1,0:T(8,128)(2,1)} %param.7, bf16[1024,3200]{1,0:T(8,128)(2,1)S(1)} %multiply_convert_fusion.clone.6), kind=kOutput, calls=%fused_computation.2 | convolution fusion | flops 26847739904 | bytes 41156608 | tf_op jit(solution)/shard_map/dot_general | solution.py:13
  169.6 0.0 reduce-scatter.2.cloned.1.call-update
  169.6 65.3 %reduce-scatter.2.cloned.1.call-done = bf16[256,4096]{1,0:T(8,128)(2,1)} async-done(((bf16[1024,4096]{1,0:T(8,128)(2,1)}), bf16[256,4096]{1,0:T(8,128)(2,1)}) %reduce-scatter.2.cloned.1.call-update) | async-done | bytes 2097168 | tf_op jit(solution)/shard_map/reduce_scatter | solution.py:14
Async XLA Ops:
  6.5 60.9 %all-gather.2.cloned.1.call-start = ((), (), s32[]{:S(2)}) async-start(), calls=%async_computation.1 | async-start | bytes 10485760 | tf_op jit(solution)/shard_map/all_gather | solution.py:9
  7.3 227.6 %reduce-scatter.2.cloned.1.call-start = ((), (), s32[]{:S(2)}) async-start(), calls=%async_computation.2 | async-start | bytes 10485760 | tf_op jit(solution)/shard_map/reduce_scatter | solution.py:14
  67.4 33.1 %copy-start = (bf16[1024,4096]{1,0:T(8,128)(2,1)S(1)}, bf16[1024,4096]{1,0:T(8,128)(2,1)}, u32[]{:S(2)}) copy-start(bf16[1024,4096]{1,0:T(8,128)(2,1)} %all-gather.2.cloned.1.call-done) | copy-start | bytes 25165828
Sparse Core Ops, SparseCore 0:
  8.9 58.5 all-gather.1
  169.7 65.1 reduce-scatter.1
where the time goes:
time: 242 us
  waiting for transfers between devices  126 us (52%)
  matrix products  102 us (42%)
  between operations  13.4 us (6%)
    reduce_scatter x1, waiting for transfers between devices, step(): return lax.psum_scatter(term, 'tp', scatter_dimension=0, tiled=True)  65.3 us
    all_gather x1, waiting for transfers between devices, step(): rows = lax.all_gather(x, 'tp', axis=0, tiled=True)  60.1 us
    dot_general x1, matrix products, step(): up = jnp.dot(rows, w_up, preferred_element_type=jnp.float32)  35.6 us
    dot_general x1, matrix products, step(): jnp.dot(hidden, w_down, preferred_element_type=jnp.float32)  33.5 us
    dot_general x1, matrix products, step(): gate = jnp.dot(rows, w_gate, preferred_element_type=jnp.float32)  33.1 us
  transfers between devices with their start and end apart: 2, of which 2 were waited for; matrix products, arithmetic and copies ran while one was open for 0% of the time, Pallas kernels for 0%

commit v1 on v0

v1 whole, which is shorter than its diff:
```python
import jax
import jax.numpy as jnp
from jax import lax
from jax.experimental import pallas as pl
from jax.experimental.pallas import tpu as pltpu
from jax.sharding import PartitionSpec as P

D = 4096
F = 3200
ROWS = 256
HALF = ROWS // 2
PIECES = 4
PIECE = HALF // PIECES
TA = 256
TB = 512
REM = F - 12 * TA
MESH = pl.DeviceIdType.MESH
BF16 = jnp.bfloat16
F32 = jnp.float32


def kernel(x_hbm, wg, wu, wd, y_hbm,
           xs, h, wr, wc, wrem, snd, o1recv, rrecv, icist, rsrecv, own,
           ring_sem, cache_sem, rem_sem, px_send, px_recv, ownx_sem,
           ag_send, ag_recv, fwd_send, fwd_recv, snd_sem, o1_sem, rr_sem,
           ici_send, rs_sem, out_sem):
    me = lax.axis_index("tp")
    cp = lax.rem(me, 2)
    partner = me + 1 - 2 * cp
    mirror = lax.rem(me + 2, 4)
    far = mirror - cp

    def remote(src, dst, ssem, rsem, dev):
        return pltpu.make_async_remote_copy(
            src_ref=src, dst_ref=dst, send_sem=ssem, recv_sem=rsem,
            device_id={"tp": dev}, device_id_type=MESH)

    def a_copies(t, dst, sems, width):
        cols = pl.ds(t * TA, width)
        return [
            pltpu.make_async_copy(wg.at[:, cols], dst.at[:, pl.ds(0, width)], sems.at[0]),
            pltpu.make_async_copy(wu.at[:, cols], dst.at[:, pl.ds(width, width)], sems.at[1]),
        ]

    def tile_of(i, q):
        return 2 * i + (1 - cp if q == 0 else cp)

    def ring_a(s, b):
        return [c for q in range(2) for c in a_copies(3 * b + q, wr.at[s, q], ring_sem.at[s, q], TA)]

    def ring_b(s, i):
        out_ = []
        for q in range(2):
            cols = pl.ds(pl.multiple_of(tile_of(i, q) * TB, TB), TB)
            out_.append(pltpu.make_async_copy(wd.at[:, cols], wr.at[s, q, pl.ds(0, F), :], ring_sem.at[s, q, 0]))
        return out_

    def cache(b):
        return a_copies(3 * b + 2, wc.at[b], cache_sem.at[b], TA)

    def rem_copies():
        return a_copies(12, wrem, rem_sem, REM)

    def start(copies):
        for c in copies:
            c.start()

    def wait(copies):
        for c in copies:
            c.wait()

    def px():
        return remote(x_hbm, xs.at[0], px_send, px_recv, partner)

    def ag(k, p):
        return remote(x_hbm.at[pl.ds(k * HALF + p * PIECE, PIECE)],
                      xs.at[1 + k, pl.ds(pl.multiple_of(cp * HALF + p * PIECE, PIECE), PIECE)],
                      ag_send.at[k, p], ag_recv.at[k, p], mirror)

    def fwd(k, p):
        rows = pl.ds(pl.multiple_of(cp * HALF + p * PIECE, PIECE), PIECE)
        return remote(xs.at[1 + k, rows], xs.at[1 + k, rows], fwd_send.at[k, p], fwd_recv.at[k, p], partner)

    def o1_copy(j):
        return remote(snd.at[j], o1recv.at[j], snd_sem.at[j], o1_sem.at[j], partner)

    def rr_copy(k, i):
        return remote(snd.at[4 * k + i], rrecv.at[k, i], snd_sem.at[4 * k + i], rr_sem.at[k, i], partner)

    def rs_copy(k, i, r):
        j = tile_of(i, 1)
        return remote(icist.at[k, i, pl.ds(r * HALF, HALF), :],
                      rsrecv.at[j, pl.ds(pl.multiple_of(k * HALF, HALF), HALF), :],
                      ici_send.at[k, i, r], rs_sem.at[k, j], far + r)

    def out_copy(slot, j):
        return pltpu.make_async_copy(
            snd.at[slot], y_hbm.at[:, pl.ds(pl.multiple_of(j * TB, TB), TB)], out_sem.at[slot])

    def ownx():
        return pltpu.make_async_copy(x_hbm, xs.at[0], ownx_sem)

    start(ring_a(0, 0))
    start(cache(0))
    start(ring_a(1, 1))
    start(cache(1))

    barrier = pltpu.get_barrier_semaphore()
    for other in (partner, mirror, mirror + 1 - 2 * cp):
        pl.semaphore_signal(barrier, inc=1, device_id={"tp": other}, device_id_type=MESH)
    pl.semaphore_wait(barrier, 3)

    px().start()
    for k in range(2):
        for p in range(PIECES):
            ag(k, p).start()
    start(cache(2))
    start(cache(3))
    start(rem_copies())

    def finish(k, i, buf):
        rr_copy(k, i).wait_recv()
        icist[k, i] = (own[buf] + rrecv[k, i].astype(F32)).astype(BF16)
        for r in range(2):
            rs_copy(k, i, r).start()

    def glu(gu, width):
        g = gu[:, :width]
        return (g * jax.nn.sigmoid(g) * gu[:, width:]).astype(BF16)

    def chunk(c, carry):
        xi = lax.rem(c, 3)

        @pl.when(c == 0)
        def _():
            px().wait_recv()

        @pl.when(c == 1)
        def _():
            ownx().start()
            for p in range(PIECES):
                fwd(0, p).wait_recv()

        @pl.when(c == 2)
        def _():
            for p in range(PIECES):
                fwd(1, p).wait_recv()

        @pl.when(c == 3)
        def _():
            ownx().wait()

        def forward(p):
            for k in range(2):
                @pl.when(c == k)
                def _():
                    ag(k, p).wait_recv()
                    fwd(k, p).start()

        for b in range(4):
            if b == 1:
                forward(0)
                for k in range(2):
                    @pl.when(c == 2 + k)
                    def _():
                        finish(k, 3, 1)
            if b == 3:
                forward(1)
            s = lax.rem(c * 8 + b, 3)
            wait(ring_a(s, b))

            @pl.when(c == 0)
            def _():
                wait(cache(b))
                if b == 3:
                    wait(rem_copies())

            s2 = lax.rem(c * 8 + b + 2, 3)
            start(ring_a(s2, b + 2) if b + 2 < 4 else ring_b(s2, b + 2 - 4))
            for q in range(3):
                w = wr[s, q] if q < 2 else wc[b]
                gu = jnp.dot(xs[xi], w, preferred_element_type=F32)
                h[:, (3 * b + q) * TA:(3 * b + q + 1) * TA] = glu(gu, TA)
            if b == 3:
                gu = jnp.dot(xs[xi], wrem[...], preferred_element_type=F32)
                h[:, 12 * TA:] = glu(gu, REM)
        forward(2)

        def ring_step(i):
            g = c * 8 + 4 + i
            s = lax.rem(g, 3)
            wait(ring_b(s, i))
            s2 = lax.rem(g + 2, 3)

            @pl.when(i < 2)
            def _():
                start(ring_b(s2, i + 2))

            for b in range(2):
                @pl.when((i == 2 + b) & (c < 3))
                def _():
                    start(ring_a(s2, b))
            return s

        def down(s, q):
            return jnp.dot(h[...], wr[s, q, pl.ds(0, F), :], preferred_element_type=F32)

        @pl.when(c == 0)
        def _():
            def step(i, carry):
                @pl.when(i == 3)
                def _():
                    forward(3)
                s = ring_step(i)
                for q in range(2):
                    snd[tile_of(i, q)] = down(s, q).astype(BF16)
                for q in range(2):
                    o1_copy(tile_of(i, q)).start()
                return carry
            lax.fori_loop(0, 4, step, 0)

        @pl.when((c == 1) | (c == 2))
        def _():
            k = c - 1

            def step(i, carry):
                @pl.when((i == 3) & (c == 1))
                def _():
                    forward(3)
                s = ring_step(i)
                o1_copy(4 * k + i).wait_send()
                snd[4 * k + i] = down(s, 0).astype(BF16)
                own[lax.rem(i, 2)] = down(s, 1)
                rr_copy(k, i).start()

                @pl.when(i > 0)
                def _():
                    finish(k, i - 1, lax.rem(i + 1, 2))
                return carry
            lax.fori_loop(0, 4, step, 0)

        @pl.when(c == 3)
        def _():
            def step(i, carry):
                s = ring_step(i)
                for q in range(2):
                    own[q] = down(s, q)
                for q in range(2):
                    j = tile_of(i, q)
                    slot = 2 * lax.rem(i, 2) + q

                    @pl.when(i < 2)
                    def _():
                        rr_copy(0, slot).wait_send()

                    @pl.when(i >= 2)
                    def _():
                        out_copy(slot, j).wait()
                    o1_copy(j).wait_recv()
                    for k in range(2):
                        rs_wait(k, j)
                    snd[slot] = (own[q] + o1recv[j].astype(F32) + rsrecv[j].astype(F32)).astype(BF16)
                    out_copy(slot, j).start()
                return carry
            lax.fori_loop(0, 4, step, 0)
        return carry

    def rs_wait(k, j):
        remote(icist.at[0, 0, pl.ds(0, HALF), :],
               rsrecv.at[j, pl.ds(k * HALF, HALF), :],
               ici_send.at[0, 0, 0], rs_sem.at[k, j], far).wait_recv()

    lax.fori_loop(0, 4, chunk, 0)

    for i in range(2):
        for q in range(2):
            out_copy(2 * i + q, tile_of(2 + i, q)).wait()
    px().wait_send()
    for k in range(2):
        for p in range(PIECES):
            ag(k, p).wait_send()
            fwd(k, p).wait_send()
        for i in range(4):
            if k == 1:
                rr_copy(k, i).wait_send()
            for r in range(2):
                rs_copy(k, i, r).wait_send()


def solution(mesh):
    def step(x, w_gate, w_up, w_down):
        dma = pltpu.SemaphoreType.DMA
        return pl.pallas_call(
            kernel,
            out_shape=jax.ShapeDtypeStruct((ROWS, D), BF16),
            in_specs=[pl.BlockSpec(memory_space=pl.ANY)] * 4,
            out_specs=pl.BlockSpec(memory_space=pl.ANY),
            scratch_shapes=[
                pltpu.VMEM((3, ROWS, D), BF16),
                pltpu.VMEM((ROWS, F), BF16),
                pltpu.VMEM((3, 2, D, 2 * TA), BF16),
                pltpu.VMEM((4, D, 2 * TA), BF16),
                pltpu.VMEM((D, 2 * REM), BF16),
                pltpu.VMEM((8, ROWS, TB), BF16),
                pltpu.VMEM((8, ROWS, TB), BF16),
                pltpu.VMEM((2, 4, ROWS, TB), BF16),
                pltpu.VMEM((2, 4, ROWS, TB), BF16),
                pltpu.VMEM((8, ROWS, TB), BF16),
                pltpu.VMEM((2, ROWS, TB), F32),
                dma((3, 2, 2)),
                dma((4, 2)),
                dma((2,)),
                dma,
                dma,
                dma,
                dma((2, PIECES)),
                dma((2, PIECES)),
                dma((2, PIECES)),
                dma((2, PIECES)),
                dma((8,)),
                dma((8,)),
                dma((2, 4)),
                dma((2, 4, 2)),
                dma((2, 8)),
                dma((4,)),
            ],
            compiler_params=pltpu.CompilerParams(
                collective_id=0, has_side_effects=True, vmem_limit_bytes=67043328),
            name="mlp_block",
        )(x, w_gate, w_up, w_down)

    return jax.shard_map(
        step,
        mesh=mesh,
        in_specs=(P(("dp", "tp"), None), P(None, "tp"), P(None, "tp"), P("tp", None)),
        out_specs=P(("dp", "tp"), None),
        check_vma=False,
    )
```

time: 242 us -> 107 us (0.44)
  waiting for transfers between devices: 126 us -> 0 us
  Pallas kernels: 0 us -> 103 us
  matrix products: 102 us -> 0 us
  between operations: 13.4 us -> 0.01 us
  local copies, waits for them, and re-layouts: 0.01 us -> 3.13 us
    pallas_call x0 -> x1, Pallas kernels: none -> 103 us  [step(): pl.pallas_call(kernel, out_shape=jax.ShapeDtypeStruct((ROWS, D), BF16), i...]
    dot_general x3 -> x0, matrix products: 102 us -> none  [the longest x1 35.6 us: step(): up = jnp.dot(rows, w_up, preferred_element_type=jnp.float32)]
    reduce_scatter x1 -> x0, waiting for transfers between devices: 65.3 us -> none  [step(): return lax.psum_scatter(term, 'tp', scatter_dimension=0, tiled=True)]
    all_gather x1 -> x0, waiting for transfers between devices: 60.1 us -> none  [step(): rows = lax.all_gather(x, 'tp', axis=0, tiled=True)]
    unnamed x2 -> x1, local copies, waits for them, and re-layouts: 0.01 us -> 3.13 us
  transfers between devices with their start and end apart: 2 -> 0, of which waited for: 2 -> 0; matrix products, arithmetic and copies ran while one was open for 0% -> 0% of each run, Pallas kernels for 0% -> 0%
where the time goes in v1:
time: 107 us; the launch traced here: 106 us
  Pallas kernels  103 us (96%)
  local copies, waits for them, and re-layouts  3.13 us (3%)
    pallas_call x1, Pallas kernels, step(): pl.pallas_call(kernel, out_shape=jax.ShapeDtypeStruct((ROWS, D), BF16), i...  103 us
    unnamed x1, local copies, waits for them, and re-layouts  3.13 us

profile of v1, /device:TPU:0, one launch (start us, length us, event | category | flops | bytes accessed | tf_op | source)
XLA Modules:
  0.0 106.5 jit_solution(6201537521556675115)
XLA Ops:
  0.0 103.3 %mlp_block.1 = bf16[256,4096]{1,0:T(8,128)(2,1)} custom-call(bf16[256,4096]{1,0:T(8,128)(2,1)} %x_hbm.1, bf16[4096,3200]{1,0:T(8,128)(2,1)} %wg.1, bf16[4096,3200]{1,0:T(8,128)(2,1)} %wu.1, bf16[3200,4096]{1,0:T(8,128)(2,1)} %wd.1), custom_call_target="tpu_custom_call" | custom-call | tf_op jit(solution)/shard_map/mlp_block/pallas_call | solution.py:293
  103.3 3.1 %copy.6 = bf16[256,4096]{1,0:T(8,128)(2,1)} copy(bf16[256,4096]{1,0:T(8,128)(2,1)} %mlp_block.1) | data formatting | bytes 4194304

commit v2 on v1

--- a/solution.py
+++ b/solution.py
@@ -15,15 +15,16 @@
 TB = 512
 REM = F - 12 * TA
 MESH = pl.DeviceIdType.MESH
+VMEM_LIMIT = 67043328 - 9 * 2 ** 18
 BF16 = jnp.bfloat16
 F32 = jnp.float32
 
 
-def kernel(x_hbm, wg, wu, wd, y_hbm,
-           xs, h, wr, wc, wrem, snd, o1recv, rrecv, icist, rsrecv, own,
+def kernel(x_hbm, wg, wu, wd, y_ref,
+           xs, h, wr, wc, wrem, snd, o1recv, rrecv, icist, own0, own1, own2,
            ring_sem, cache_sem, rem_sem, px_send, px_recv, ownx_sem,
            ag_send, ag_recv, fwd_send, fwd_recv, snd_sem, o1_sem, rr_sem,
-           ici_send, rs_sem, out_sem):
+           ici_send, rs_sem, credit):
     me = lax.axis_index("tp")
     cp = lax.rem(me, 2)
     partner = me + 1 - 2 * cp
@@ -42,6 +43,9 @@
             pltpu.make_async_copy(wu.at[:, cols], dst.at[:, pl.ds(width, width)], sems.at[1]),
         ]
 
+    def tile_cols(j):
+        return pl.ds(pl.multiple_of(j * TB, TB), TB)
+
     def tile_of(i, q):
         return 2 * i + (1 - cp if q == 0 else cp)
 
@@ -81,21 +85,17 @@
         rows = pl.ds(pl.multiple_of(cp * HALF + p * PIECE, PIECE), PIECE)
         return remote(xs.at[1 + k, rows], xs.at[1 + k, rows], fwd_send.at[k, p], fwd_recv.at[k, p], partner)
 
-    def o1_copy(j):
-        return remote(snd.at[j], o1recv.at[j], snd_sem.at[j], o1_sem.at[j], partner)
+    def o1_copy(slot, j):
+        return remote(snd.at[slot], o1recv.at[j], snd_sem.at[slot], o1_sem.at[j], partner)
 
     def rr_copy(k, i):
-        return remote(snd.at[4 * k + i], rrecv.at[k, i], snd_sem.at[4 * k + i], rr_sem.at[k, i], partner)
+        return remote(snd.at[i], rrecv.at[k, i], snd_sem.at[i], rr_sem.at[k, i], partner)
 
     def rs_copy(k, i, r):
         j = tile_of(i, 1)
         return remote(icist.at[k, i, pl.ds(r * HALF, HALF), :],
-                      rsrecv.at[j, pl.ds(pl.multiple_of(k * HALF, HALF), HALF), :],
+                      xs.at[1, pl.ds(pl.multiple_of(k * HALF, HALF), HALF), tile_cols(j)],
                       ici_send.at[k, i, r], rs_sem.at[k, j], far + r)
-
-    def out_copy(slot, j):
-        return pltpu.make_async_copy(
-            snd.at[slot], y_hbm.at[:, pl.ds(pl.multiple_of(j * TB, TB), TB)], out_sem.at[slot])
 
     def ownx():
         return pltpu.make_async_copy(x_hbm, xs.at[0], ownx_sem)
@@ -118,9 +118,12 @@
     start(cache(3))
     start(rem_copies())
 
-    def finish(k, i, buf):
-        rr_copy(k, i).wait_recv()
-        icist[k, i] = (own[buf] + rrecv[k, i].astype(F32)).astype(BF16)
+    own = (own0, own1, own2)
+
+    def pair_sum(k, i):
+        icist[k, i] = (own[i % 3][...] + rrecv[k, i].astype(F32)).astype(BF16)
+
+    def pair_send(k, i):
         for r in range(2):
             rs_copy(k, i, r).start()
 
@@ -163,7 +166,10 @@
                 for k in range(2):
                     @pl.when(c == 2 + k)
                     def _():
-                        finish(k, 3, 1)
+                        for i in (2, 3):
+                            rr_copy(k, i).wait_recv()
+                            pair_sum(k, i)
+                            pair_send(k, i)
             if b == 3:
                 forward(1)
             s = lax.rem(c * 8 + b, 3)
@@ -186,20 +192,24 @@
                 h[:, 12 * TA:] = glu(gu, REM)
         forward(2)
 
+        @pl.when(c == 1)
+        def _():
+            for p in range(PIECES):
+                fwd(0, p).wait_send()
+            for r in range(2):
+                pl.semaphore_signal(credit, inc=1, device_id={"tp": far + r}, device_id_type=MESH)
+
         def ring_step(i):
             g = c * 8 + 4 + i
             s = lax.rem(g, 3)
             wait(ring_b(s, i))
             s2 = lax.rem(g + 2, 3)
-
-            @pl.when(i < 2)
-            def _():
+            if i < 2:
                 start(ring_b(s2, i + 2))
-
-            for b in range(2):
-                @pl.when((i == 2 + b) & (c < 3))
+            else:
+                @pl.when(c < 3)
                 def _():
-                    start(ring_a(s2, b))
+                    start(ring_a(s2, i - 2))
             return s
 
         def down(s, q):
@@ -207,79 +217,83 @@
 
         @pl.when(c == 0)
         def _():
-            def step(i, carry):
-                @pl.when(i == 3)
-                def _():
+            for i in range(4):
+                if i == 3:
                     forward(3)
                 s = ring_step(i)
+                slots = [2 * (i % 2) + q for q in range(2)]
+                if i >= 2:
+                    for q in range(2):
+                        o1_copy(slots[q], tile_of(i, q)).wait_send()
                 for q in range(2):
-                    snd[tile_of(i, q)] = down(s, q).astype(BF16)
+                    snd[slots[q]] = down(s, q).astype(BF16)
                 for q in range(2):
-                    o1_copy(tile_of(i, q)).start()
-                return carry
-            lax.fori_loop(0, 4, step, 0)
+                    o1_copy(slots[q], tile_of(i, q)).start()
 
         @pl.when((c == 1) | (c == 2))
         def _():
             k = c - 1
-
-            def step(i, carry):
-                @pl.when((i == 3) & (c == 1))
-                def _():
-                    forward(3)
+            for i in range(4):
+                if i == 3:
+                    @pl.when(c == 1)
+                    def _():
+                        forward(3)
                 s = ring_step(i)
-                o1_copy(4 * k + i).wait_send()
-                snd[4 * k + i] = down(s, 0).astype(BF16)
-                own[lax.rem(i, 2)] = down(s, 1)
+                rr_copy(k, i).wait_send()
+                if i >= 2:
+                    rr_copy(k, i - 2).wait_recv()
+                    pair_sum(k, i - 2)
+                snd[i] = down(s, 0).astype(BF16)
+                own[i % 3][...] = down(s, 1)
                 rr_copy(k, i).start()
-
-                @pl.when(i > 0)
-                def _():
-                    finish(k, i - 1, lax.rem(i + 1, 2))
-                return carry
-            lax.fori_loop(0, 4, step, 0)
+                if i == 2:
+                    @pl.when(c == 1)
+                    def _():
+                        pl.semaphore_wait(credit, 2)
+                if i >= 2:
+                    pair_send(k, i - 2)
 
         @pl.when(c == 3)
         def _():
-            def step(i, carry):
-                s = ring_step(i)
-                for q in range(2):
-                    own[q] = down(s, q)
+            def arrive(i):
                 for q in range(2):
                     j = tile_of(i, q)
-                    slot = 2 * lax.rem(i, 2) + q
-
-                    @pl.when(i < 2)
-                    def _():
-                        rr_copy(0, slot).wait_send()
-
-                    @pl.when(i >= 2)
-                    def _():
-                        out_copy(slot, j).wait()
-                    o1_copy(j).wait_recv()
+                    o1_copy(0, j).wait_recv()
                     for k in range(2):
                         rs_wait(k, j)
-                    snd[slot] = (own[q] + o1recv[j].astype(F32) + rsrecv[j].astype(F32)).astype(BF16)
-                    out_copy(slot, j).start()
-                return carry
-            lax.fori_loop(0, 4, step, 0)
+
+            def total(i, q, mine):
+                j = tile_of(i, q)
+                cols = tile_cols(j)
+                y_ref[:, cols] = (mine + o1recv[j].astype(F32) + xs[1, :, cols].astype(F32)).astype(BF16)
+
+            for i in range(4):
+                s = ring_step(i)
+                if i < 3:
+                    arrive(i)
+                    for q in range(2):
+                        total(i, q, down(s, q))
+                else:
+                    for q in range(2):
+                        own[q][...] = down(s, q)
+                    arrive(i)
+                    for q in range(2):
+                        total(i, q, own[q][...])
         return carry
 
     def rs_wait(k, j):
         remote(icist.at[0, 0, pl.ds(0, HALF), :],
-               rsrecv.at[j, pl.ds(k * HALF, HALF), :],
+               xs.at[1, pl.ds(k * HALF, HALF), tile_cols(j)],
                ici_send.at[0, 0, 0], rs_sem.at[k, j], far).wait_recv()
 
     lax.fori_loop(0, 4, chunk, 0)
 
-    for i in range(2):
-        for q in range(2):
-            out_copy(2 * i + q, tile_of(2 + i, q)).wait()
     px().wait_send()
     for k in range(2):
         for p in range(PIECES):
             ag(k, p).wait_send()
-            fwd(k, p).wait_send()
+            if k == 1:
+                fwd(k, p).wait_send()
         for i in range(4):
             if k == 1:
                 rr_copy(k, i).wait_send()
@@ -292,21 +306,22 @@
         dma = pltpu.SemaphoreType.DMA
         return pl.pallas_call(
             kernel,
-            out_shape=jax.ShapeDtypeStruct((ROWS, D), BF16),
+            out_shape=pltpu.VMEM((ROWS, D), BF16),
             in_specs=[pl.BlockSpec(memory_space=pl.ANY)] * 4,
-            out_specs=pl.BlockSpec(memory_space=pl.ANY),
+            out_specs=pl.BlockSpec(memory_space=pltpu.VMEM),
             scratch_shapes=[
                 pltpu.VMEM((3, ROWS, D), BF16),
                 pltpu.VMEM((ROWS, F), BF16),
                 pltpu.VMEM((3, 2, D, 2 * TA), BF16),
                 pltpu.VMEM((4, D, 2 * TA), BF16),
                 pltpu.VMEM((D, 2 * REM), BF16),
-                pltpu.VMEM((8, ROWS, TB), BF16),
+                pltpu.VMEM((4, ROWS, TB), BF16),
                 pltpu.VMEM((8, ROWS, TB), BF16),
                 pltpu.VMEM((2, 4, ROWS, TB), BF16),
                 pltpu.VMEM((2, 4, ROWS, TB), BF16),
-                pltpu.VMEM((8, ROWS, TB), BF16),
-                pltpu.VMEM((2, ROWS, TB), F32),
+                pltpu.VMEM((ROWS, TB), F32),
+                pltpu.VMEM((ROWS, TB), F32),
+                pltpu.VMEM((ROWS, TB), F32),
                 dma((3, 2, 2)),
                 dma((4, 2)),
                 dma((2,)),
@@ -317,15 +332,15 @@
                 dma((2, PIECES)),
                 dma((2, PIECES)),
                 dma((2, PIECES)),
-                dma((8,)),
+                dma((4,)),
                 dma((8,)),
                 dma((2, 4)),
                 dma((2, 4, 2)),
                 dma((2, 8)),
-                dma((4,)),
+                pltpu.SemaphoreType.REGULAR,
             ],
             compiler_params=pltpu.CompilerParams(
-                collective_id=0, has_side_effects=True, vmem_limit_bytes=67043328),
+                collective_id=0, has_side_effects=True, vmem_limit_bytes=VMEM_LIMIT),
             name="mlp_block",
         )(x, w_gate, w_up, w_down)
 

time: 107 us -> 103 us (0.963)
  local copies, waits for them, and re-layouts: 3.13 us -> 1.32 us
    unnamed x1, local copies, waits for them, and re-layouts: 3.13 us -> 1.32 us
    pallas_call x1, Pallas kernels: 103 us -> 102 us  [step(): pl.pallas_call(kernel, out_shape=pltpu.VMEM((ROWS, D), BF16), in_specs=[p...]
where the time goes in v2:
time: 103 us
  Pallas kernels  102 us (99%)
  local copies, waits for them, and re-layouts  1.32 us (1%)
    pallas_call x1, Pallas kernels, step(): pl.pallas_call(kernel, out_shape=pltpu.VMEM((ROWS, D), BF16), in_specs=[p...  102 us

profile of v2, /device:TPU:0, one launch (start us, length us, event | category | flops | bytes accessed | tf_op | source)
XLA Modules:
  0.0 103.1 jit_solution(4734653328443778440)
XLA Ops:
  0.0 101.8 %mlp_block.1 = bf16[256,4096]{1,0:T(8,128)(2,1)S(1)} custom-call(bf16[256,4096]{1,0:T(8,128)(2,1)} %x_hbm.1, bf16[4096,3200]{1,0:T(8,128)(2,1)} %wg.1, bf16[4096,3200]{1,0:T(8,128)(2,1)} %wu.1, bf16[3200,4096]{1,0:T(8,128)(2,1)} %wd.1), custom_call_target="tpu_custom_call" | custom-call | tf_op jit(solution)/shard_map/mlp_block/pallas_call | solution.py:307
  101.8 1.3 %copy.6 = bf16[256,4096]{1,0:T(8,128)(2,1)} copy(bf16[256,4096]{1,0:T(8,128)(2,1)S(1)} %mlp_block.1) | data formatting | bytes 4194304

commit v3 on v2

--- a/solution.py
+++ b/solution.py
@@ -37,7 +37,7 @@
             device_id={"tp": dev}, device_id_type=MESH)
 
     def a_copies(t, dst, sems, width):
-        cols = pl.ds(t * TA, width)
+        cols = pl.ds(pl.multiple_of(t * TA, TA), width)
         return [
             pltpu.make_async_copy(wg.at[:, cols], dst.at[:, pl.ds(0, width)], sems.at[0]),
             pltpu.make_async_copy(wu.at[:, cols], dst.at[:, pl.ds(width, width)], sems.at[1]),
@@ -160,8 +160,13 @@
                     ag(k, p).wait_recv()
                     fwd(k, p).start()
 
-        for b in range(4):
-            if b == 1:
+        def tile(t, w, width):
+            gu = jnp.dot(xs[xi], w, preferred_element_type=F32)
+            h[:, pl.ds(pl.multiple_of(t * TA, TA), width)] = glu(gu, width)
+
+        def block(b, carry):
+            @pl.when(b == 1)
+            def _():
                 forward(0)
                 for k in range(2):
                     @pl.when(c == 2 + k)
@@ -170,26 +175,38 @@
                             rr_copy(k, i).wait_recv()
                             pair_sum(k, i)
                             pair_send(k, i)
-            if b == 3:
-                forward(1)
             s = lax.rem(c * 8 + b, 3)
             wait(ring_a(s, b))
 
             @pl.when(c == 0)
             def _():
                 wait(cache(b))
-                if b == 3:
-                    wait(rem_copies())
-
             s2 = lax.rem(c * 8 + b + 2, 3)
-            start(ring_a(s2, b + 2) if b + 2 < 4 else ring_b(s2, b + 2 - 4))
+
+            @pl.when(b < 2)
+            def _():
+                start(ring_a(s2, b + 2))
+
+            @pl.when(b == 2)
+            def _():
+                start(ring_b(s2, 0))
             for q in range(3):
-                w = wr[s, q] if q < 2 else wc[b]
-                gu = jnp.dot(xs[xi], w, preferred_element_type=F32)
-                h[:, (3 * b + q) * TA:(3 * b + q + 1) * TA] = glu(gu, TA)
-            if b == 3:
-                gu = jnp.dot(xs[xi], wrem[...], preferred_element_type=F32)
-                h[:, 12 * TA:] = glu(gu, REM)
+                tile(3 * b + q, wr[s, q] if q < 2 else wc[b], TA)
+            return carry
+
+        lax.fori_loop(0, 3, block, 0)
+        forward(1)
+        s = lax.rem(c * 8 + 3, 3)
+        wait(ring_a(s, 3))
+
+        @pl.when(c == 0)
+        def _():
+            wait(cache(3))
+            wait(rem_copies())
+        start(ring_b(lax.rem(c * 8 + 5, 3), 1))
+        for q in range(3):
+            tile(9 + q, wr[s, q] if q < 2 else wc[3], TA)
+        tile(12, wrem[...], REM)
         forward(2)
 
         @pl.when(c == 1)

time: 103 us -> 101 us (0.981); the launches traced: 103 us -> 99.5 us
  Pallas kernels: 102 us -> 98.2 us
    pallas_call x1, Pallas kernels: 102 us -> 98.2 us  [step(): pl.pallas_call(kernel, out_shape=pltpu.VMEM((ROWS, D), BF16), in_specs=[p...]
where the time goes in v3:
time: 101 us; the launch traced here: 99.5 us
  Pallas kernels  98.2 us (97%)
  local copies, waits for them, and re-layouts  1.32 us (1%)
    pallas_call x1, Pallas kernels, step(): pl.pallas_call(kernel, out_shape=pltpu.VMEM((ROWS, D), BF16), in_specs=[p...  98.2 us

profile of v3, /device:TPU:0, one launch (start us, length us, event | category | flops | bytes accessed | tf_op | source)
XLA Modules:
  0.0 99.5 jit_solution(7934871012484588698)
XLA Ops:
  0.0 98.2 %mlp_block.1 = bf16[256,4096]{1,0:T(8,128)(2,1)S(1)} custom-call(bf16[256,4096]{1,0:T(8,128)(2,1)} %x_hbm.1, bf16[4096,3200]{1,0:T(8,128)(2,1)} %wg.1, bf16[4096,3200]{1,0:T(8,128)(2,1)} %wu.1, bf16[3200,4096]{1,0:T(8,128)(2,1)} %wd.1), custom_call_target="tpu_custom_call" | custom-call | tf_op jit(solution)/shard_map/mlp_block/pallas_call | solution.py:324
  98.2 1.3 %copy.6 = bf16[256,4096]{1,0:T(8,128)(2,1)} copy(bf16[256,4096]{1,0:T(8,128)(2,1)S(1)} %mlp_block.1) | data formatting | bytes 4194304

commit v4 on v3

--- a/solution.py
+++ b/solution.py
@@ -21,10 +21,10 @@
 
 
 def kernel(x_hbm, wg, wu, wd, y_ref,
-           xs, h, wr, wc, wrem, snd, o1recv, rrecv, icist, own0, own1, own2,
+           xs, h, hown, wr, wc, wrem, snd, o1recv, rrecv, icist, own0, own1,
            ring_sem, cache_sem, rem_sem, px_send, px_recv, ownx_sem,
            ag_send, ag_recv, fwd_send, fwd_recv, snd_sem, o1_sem, rr_sem,
-           ici_send, rs_sem, credit):
+           ici_send, rs_sem, credit, free):
     me = lax.axis_index("tp")
     cp = lax.rem(me, 2)
     partner = me + 1 - 2 * cp
@@ -49,13 +49,18 @@
     def tile_of(i, q):
         return 2 * i + (1 - cp if q == 0 else cp)
 
+    def down_tile(c, i, q):
+        last = c // 3
+        other = 2 * (2 * (i // 2) + q) + (1 - cp if i % 2 == 0 else cp)
+        return last * tile_of(i, q) + (1 - last) * other
+
     def ring_a(s, b):
         return [c for q in range(2) for c in a_copies(3 * b + q, wr.at[s, q], ring_sem.at[s, q], TA)]
 
-    def ring_b(s, i):
+    def ring_b(c, s, i):
         out_ = []
         for q in range(2):
-            cols = pl.ds(pl.multiple_of(tile_of(i, q) * TB, TB), TB)
+            cols = tile_cols(down_tile(c, i, q))
             out_.append(pltpu.make_async_copy(wd.at[:, cols], wr.at[s, q, pl.ds(0, F), :], ring_sem.at[s, q, 0]))
         return out_
 
@@ -67,7 +72,7 @@
 
     def start(copies):
         for c in copies:
-            c.start()
+            c.start(priority=1)
 
     def wait(copies):
         for c in copies:
@@ -97,13 +102,12 @@
                       xs.at[1, pl.ds(pl.multiple_of(k * HALF, HALF), HALF), tile_cols(j)],
                       ici_send.at[k, i, r], rs_sem.at[k, j], far + r)
 
-    def ownx():
-        return pltpu.make_async_copy(x_hbm, xs.at[0], ownx_sem)
-
+    def ownx(slot):
+        return pltpu.make_async_copy(x_hbm, xs.at[slot], ownx_sem)
+
+    ownx(2).start()
     start(ring_a(0, 0))
     start(cache(0))
-    start(ring_a(1, 1))
-    start(cache(1))
 
     barrier = pltpu.get_barrier_semaphore()
     for other in (partner, mirror, mirror + 1 - 2 * cp):
@@ -111,17 +115,13 @@
     pl.semaphore_wait(barrier, 3)
 
     px().start()
-    for k in range(2):
-        for p in range(PIECES):
-            ag(k, p).start()
-    start(cache(2))
-    start(cache(3))
-    start(rem_copies())
-
-    own = (own0, own1, own2)
+    for p in range(PIECES):
+        ag(0, p).start()
+
+    own = (own0, own1)
 
     def pair_sum(k, i):
-        icist[k, i] = (own[i % 3][...] + rrecv[k, i].astype(F32)).astype(BF16)
+        icist[k, i] = (own[i % 2][...] + rrecv[k, i].astype(F32)).astype(BF16)
 
     def pair_send(k, i):
         for r in range(2):
@@ -131,8 +131,18 @@
         g = gu[:, :width]
         return (g * jax.nn.sigmoid(g) * gu[:, width:]).astype(BF16)
 
+    first = ring_a(0, 0)
+    ownx(2).wait()
+    for q in range(3):
+        wait(first[2 * q:2 * q + 2] if q < 2 else cache(0))
+        start((ring_a(1, 1), cache(1), ring_a(2, 2))[q])
+        gu = jnp.dot(xs[2], wr[0, q] if q < 2 else wc[0], preferred_element_type=F32)
+        hown[:, q * TA:(q + 1) * TA] = glu(gu, TA)
+    pl.semaphore_signal(free, inc=1, device_id={"tp": mirror}, device_id_type=MESH)
+
     def chunk(c, carry):
         xi = lax.rem(c, 3)
+        skip = c // 3
 
         @pl.when(c == 0)
         def _():
@@ -140,7 +150,7 @@
 
         @pl.when(c == 1)
         def _():
-            ownx().start()
+            ownx(0).start()
             for p in range(PIECES):
                 fwd(0, p).wait_recv()
 
@@ -151,7 +161,8 @@
 
         @pl.when(c == 3)
         def _():
-            ownx().wait()
+            ownx(0).wait()
+            h[:, :3 * TA] = hown[...]
 
         def forward(p):
             for k in range(2):
@@ -164,46 +175,59 @@
             gu = jnp.dot(xs[xi], w, preferred_element_type=F32)
             h[:, pl.ds(pl.multiple_of(t * TA, TA), width)] = glu(gu, width)
 
+        def slot_of(n):
+            return lax.rem(c * 8 + n - skip, 3)
+
         def block(b, carry):
             @pl.when(b == 1)
             def _():
                 forward(0)
-                for k in range(2):
-                    @pl.when(c == 2 + k)
-                    def _():
-                        for i in (2, 3):
-                            rr_copy(k, i).wait_recv()
-                            pair_sum(k, i)
-                            pair_send(k, i)
-            s = lax.rem(c * 8 + b, 3)
-            wait(ring_a(s, b))
-
-            @pl.when(c == 0)
+
+            @pl.when((b == 1) & (c == 0))
+            def _():
+                pl.semaphore_wait(free, 1)
+                for p in range(PIECES):
+                    ag(1, p).start()
+            s = slot_of(b)
+
+            @pl.when(c + b > 0)
+            def _():
+                wait(ring_a(s, b))
+
+            @pl.when((c == 0) & (b > 0))
             def _():
                 wait(cache(b))
-            s2 = lax.rem(c * 8 + b + 2, 3)
-
-            @pl.when(b < 2)
+
+            @pl.when((c == 0) & (b < 2))
+            def _():
+                start(cache(b + 2))
+
+            @pl.when((c == 0) & (b == 1))
+            def _():
+                start(rem_copies())
+            s2 = slot_of(b + 2)
+
+            @pl.when((b < 2) & (c + b > 0))
             def _():
                 start(ring_a(s2, b + 2))
 
             @pl.when(b == 2)
             def _():
-                start(ring_b(s2, 0))
+                start(ring_b(c, s2, 0))
             for q in range(3):
                 tile(3 * b + q, wr[s, q] if q < 2 else wc[b], TA)
             return carry
 
-        lax.fori_loop(0, 3, block, 0)
+        lax.fori_loop(skip, 3, block, 0)
         forward(1)
-        s = lax.rem(c * 8 + 3, 3)
+        s = slot_of(3)
         wait(ring_a(s, 3))
 
         @pl.when(c == 0)
         def _():
             wait(cache(3))
             wait(rem_copies())
-        start(ring_b(lax.rem(c * 8 + 5, 3), 1))
+        start(ring_b(c, slot_of(5), 1))
         for q in range(3):
             tile(9 + q, wr[s, q] if q < 2 else wc[3], TA)
         tile(12, wrem[...], REM)
@@ -217,16 +241,15 @@
                 pl.semaphore_signal(credit, inc=1, device_id={"tp": far + r}, device_id_type=MESH)
 
         def ring_step(i):
-            g = c * 8 + 4 + i
-            s = lax.rem(g, 3)
-            wait(ring_b(s, i))
-            s2 = lax.rem(g + 2, 3)
+            s = slot_of(4 + i)
+            wait(ring_b(c, s, i))
+            s2 = slot_of(6 + i)
             if i < 2:
-                start(ring_b(s2, i + 2))
+                start(ring_b(c, s2, i + 2))
             else:
                 @pl.when(c < 3)
                 def _():
-                    start(ring_a(s2, i - 2))
+                    start(ring_a(s2, i - 2 + c // 2))
             return s
 
         def down(s, q):
@@ -241,11 +264,11 @@
                 slots = [2 * (i % 2) + q for q in range(2)]
                 if i >= 2:
                     for q in range(2):
-                        o1_copy(slots[q], tile_of(i, q)).wait_send()
+                        o1_copy(slots[q], down_tile(c, i, q)).wait_send()
                 for q in range(2):
                     snd[slots[q]] = down(s, q).astype(BF16)
                 for q in range(2):
-                    o1_copy(slots[q], tile_of(i, q)).start()
+                    o1_copy(slots[q], down_tile(c, i, q)).start()
 
         @pl.when((c == 1) | (c == 2))
         def _():
@@ -256,19 +279,25 @@
                     def _():
                         forward(3)
                 s = ring_step(i)
-                rr_copy(k, i).wait_send()
-                if i >= 2:
-                    rr_copy(k, i - 2).wait_recv()
-                    pair_sum(k, i - 2)
-                snd[i] = down(s, 0).astype(BF16)
-                own[i % 3][...] = down(s, 1)
-                rr_copy(k, i).start()
-                if i == 2:
-                    @pl.when(c == 1)
-                    def _():
-                        pl.semaphore_wait(credit, 2)
-                if i >= 2:
-                    pair_send(k, i - 2)
+                pairs = (2 * (i // 2), 2 * (i // 2) + 1)
+                if i % 2 == 0:
+                    for p in pairs:
+                        rr_copy(k, p).wait_send()
+                    for q, p in enumerate(pairs):
+                        snd[p] = down(s, q).astype(BF16)
+                    for p in pairs:
+                        rr_copy(k, p).start()
+                else:
+                    for q in range(2):
+                        own[q][...] = down(s, q)
+                    if i == 1:
+                        @pl.when(c == 1)
+                        def _():
+                            pl.semaphore_wait(credit, 2)
+                    for p in pairs:
+                        rr_copy(k, p).wait_recv()
+                        pair_sum(k, p)
+                        pair_send(k, p)
 
         @pl.when(c == 3)
         def _():
@@ -329,6 +358,7 @@
             scratch_shapes=[
                 pltpu.VMEM((3, ROWS, D), BF16),
                 pltpu.VMEM((ROWS, F), BF16),
+                pltpu.VMEM((ROWS, 3 * TA), BF16),
                 pltpu.VMEM((3, 2, D, 2 * TA), BF16),
                 pltpu.VMEM((4, D, 2 * TA), BF16),
                 pltpu.VMEM((D, 2 * REM), BF16),
@@ -336,7 +366,6 @@
                 pltpu.VMEM((8, ROWS, TB), BF16),
                 pltpu.VMEM((2, 4, ROWS, TB), BF16),
                 pltpu.VMEM((2, 4, ROWS, TB), BF16),
-                pltpu.VMEM((ROWS, TB), F32),
                 pltpu.VMEM((ROWS, TB), F32),
                 pltpu.VMEM((ROWS, TB), F32),
                 dma((3, 2, 2)),
@@ -355,6 +384,7 @@
                 dma((2, 4, 2)),
                 dma((2, 8)),
                 pltpu.SemaphoreType.REGULAR,
+                pltpu.SemaphoreType.REGULAR,
             ],
             compiler_params=pltpu.CompilerParams(
                 collective_id=0, has_side_effects=True, vmem_limit_bytes=VMEM_LIMIT),

time: 101 us -> 99 us (0.980)
  Pallas kernels: 98.2 us -> 96.1 us
    pallas_call x1, Pallas kernels: 98.2 us -> 96.1 us  [step(): pl.pallas_call(kernel, out_shape=pltpu.VMEM((ROWS, D), BF16), in_specs=[p...]
where the time goes in v4:
time: 99 us; the launch traced here: 97.5 us
  Pallas kernels  96.1 us (97%)
  local copies, waits for them, and re-layouts  1.32 us (1%)
    pallas_call x1, Pallas kernels, step(): pl.pallas_call(kernel, out_shape=pltpu.VMEM((ROWS, D), BF16), in_specs=[p...  96.1 us

profile of v4, /device:TPU:0, one launch (start us, length us, event | category | flops | bytes accessed | tf_op | source)
XLA Modules:
  0.0 97.5 jit_solution(7184338794968890843)
XLA Ops:
  0.0 96.1 %mlp_block.1 = bf16[256,4096]{1,0:T(8,128)(2,1)S(1)} custom-call(bf16[256,4096]{1,0:T(8,128)(2,1)} %x_hbm.1, bf16[4096,3200]{1,0:T(8,128)(2,1)} %wg.1, bf16[4096,3200]{1,0:T(8,128)(2,1)} %wu.1, bf16[3200,4096]{1,0:T(8,128)(2,1)} %wd.1), custom_call_target="tpu_custom_call" | custom-call | tf_op jit(solution)/shard_map/mlp_block/pallas_call | solution.py:353
  96.2 1.3 %copy.6 = bf16[256,4096]{1,0:T(8,128)(2,1)} copy(bf16[256,4096]{1,0:T(8,128)(2,1)S(1)} %mlp_block.1) | data formatting | bytes 4194304

commit v5 on v4

--- a/solution.py
+++ b/solution.py
@@ -105,18 +105,18 @@
     def ownx(slot):
         return pltpu.make_async_copy(x_hbm, xs.at[slot], ownx_sem)
 
-    ownx(2).start()
-    start(ring_a(0, 0))
-    start(cache(0))
-
     barrier = pltpu.get_barrier_semaphore()
     for other in (partner, mirror, mirror + 1 - 2 * cp):
         pl.semaphore_signal(barrier, inc=1, device_id={"tp": other}, device_id_type=MESH)
+
+    ownx(2).start()
+    start(ring_a(0, 0))
     pl.semaphore_wait(barrier, 3)
-
-    px().start()
     for p in range(PIECES):
         ag(0, p).start()
+    px().start()
+    start(cache(0))
+
 
     own = (own0, own1)
 

time: 99 us -> 98.4 us (level)
  no operation moved by 1% of the time
where the time goes in v5:
time: 98.4 us; the launch traced here: 96.9 us
  Pallas kernels  95.5 us (97%)
  local copies, waits for them, and re-layouts  1.32 us (1%)
    pallas_call x1, Pallas kernels, step(): pl.pallas_call(kernel, out_shape=pltpu.VMEM((ROWS, D), BF16), in_specs=[p...  95.5 us

profile of v5, /device:TPU:0, one launch (start us, length us, event | category | flops | bytes accessed | tf_op | source)
XLA Modules:
  0.0 96.9 jit_solution(7082454021489560689)
XLA Ops:
  0.0 95.5 %mlp_block.1 = bf16[256,4096]{1,0:T(8,128)(2,1)S(1)} custom-call(bf16[256,4096]{1,0:T(8,128)(2,1)} %x_hbm.1, bf16[4096,3200]{1,0:T(8,128)(2,1)} %wg.1, bf16[4096,3200]{1,0:T(8,128)(2,1)} %wu.1, bf16[3200,4096]{1,0:T(8,128)(2,1)} %wd.1), custom_call_target="tpu_custom_call" | custom-call | tf_op jit(solution)/shard_map/mlp_block/pallas_call | solution.py:353
  95.5 1.3 %copy.6 = bf16[256,4096]{1,0:T(8,128)(2,1)} copy(bf16[256,4096]{1,0:T(8,128)(2,1)S(1)} %mlp_block.1) | data formatting | bytes 4194304
